TPU v7x, 128 devices: a whole 4x4x4 slice. The times are simulated.
128 devices in a mesh: grp: 4 (over z), seq: 32 (over x, y, core).
Axes of the slice: x: 4, y: 4, z: 4, core: 2. Of those that a mesh axis runs over, the one named last changes fastest.
Arguments:
- latent: bfloat16 [4, 4096, 32, 256], P('grp', 'seq'), may hold values from -6 to 6
- up_key: bfloat16 [4, 128, 256], replicated, may hold values from -0.5 to 0.5
- up_value: bfloat16 [4, 128, 256], replicated, may hold values from -0.5 to 0.5
- queries: bfloat16 [8, 64, 128], replicated, may hold values from -240 to 240, as said below
- lengths: int32 [8], replicated, may hold values from 1 to 16384
- block_dest: int32 [4096], replicated, may hold values from 0 to 127, as said below
Outputs:
- decode_latent: bfloat16 [128, 4, 32, 32, 256], P(('grp', 'seq'))
- attended: float32 [8, 8192], replicated
Inputs may be any that keep to these rules, and one draw needn't show every extreme that they name: `block_dest`: each aligned run of 128 entries (the blocks of one seq index in the prefill layout) names every decode device exactly once. `queries`: the new token's query entries, real-valued.
All inputs are finite; a program needn't handle non-finite values.
Results may differ from a plain program's by a relative error of at most 0.001.
Values may be sent and summed in bfloat16 or wider, within the bound.
A program may use at most 64 MiB of HBM per device.

v0:
```python
import jax
import jax.numpy as jnp
from jax import lax
from jax.sharding import Mesh
from jax.sharding import PartitionSpec as P

SEQ = ("seq_0", "seq_1", "seq_2")
GRP_SEQ = ("grp", "seq_0", "seq_1", "seq_2")


def all_in_one(x, axis):
    leaves = jax.tree.leaves(x)
    turns = sorted(range(len(leaves)), key=lambda k: -leaves[k].size)
    width = (1, *leaves[turns[0]].shape)[-1]
    lines = [
        jnp.pad(leaves[k].reshape(-1), (0, -leaves[k].size % width)).reshape(-1, width)
        for k in turns
    ]
    both, at, found = (lax.all_gather(jnp.concatenate(lines), axis), 0, {})
    for k, line in zip(turns, lines):
        slab = both[:, at : at + len(line)].reshape(len(both), -1)
        found[k] = slab[:, : leaves[k].size].reshape(-1, *leaves[k].shape)
        at += len(line)
    numbers = iter(range(len(leaves)))
    return jax.tree.map(lambda _: found[next(numbers)], x)


def joined_all(x, axes, combine):
    for axis in axes:
        pieces = all_in_one(x, axis)
        x = jax.tree.map(lambda part: part[0], pieces)
        for k in range(1, lax.axis_size(axis)):
            x = combine(x, jax.tree.map(lambda part: part[k], pieces))
    return x


def combine(first, second):
    largest = jnp.maximum(first[0], second[0])
    factor_a = jnp.exp(first[0] - largest)
    factor_b = jnp.exp(second[0] - largest)
    totals = first[1] * factor_a + second[1] * factor_b
    accum = first[2] * factor_a[..., None] + second[2] * factor_b[..., None]
    return (largest, totals, accum)


def slot_info(global_ids, lengths, block_len, blk_seq, batch):
    seq_ids = global_ids // blk_seq
    starts = global_ids % blk_seq * block_len
    positions = starts[:, None] + jnp.arange(block_len, dtype=jnp.int32)[None, :]
    seq_hot = (seq_ids[:, None] == jnp.arange(batch, dtype=jnp.int32)[None, :]).astype(jnp.int32)
    slot_len = jnp.sum(seq_hot * lengths[None, :], axis=1)
    live = positions < slot_len[:, None]
    return (seq_hot, live)


def partials(cache, key_map, value_map, slot_query, live, seq_hot):
    rank = cache.shape[3] // 2
    head_dim = slot_query.shape[-1]
    scale = 1.0 / float(head_dim) ** 0.5
    highest = lax.Precision.HIGHEST
    key_lat = cache[..., :rank]
    value_lat = cache[..., rank:]
    keys = jnp.einsum("gstr,grkd->gstkd", key_lat, key_map, preferred_element_type=jnp.float32)
    scores = (
        jnp.einsum("gstkd,sgkjd->gskjt", keys, slot_query.astype(jnp.float32), precision=highest)
        * scale
    )
    live_wide = live[None, :, None, None, :]
    scores = jnp.where(live_wide, scores, -1e30)
    slot_max = jnp.max(scores, axis=-1)
    weights = jnp.where(live_wide, jnp.exp(scores - slot_max[..., None]), 0.0)
    slot_tot = jnp.sum(weights, axis=-1)
    values = jnp.einsum(
        "gstr,grkd->gstkd", value_lat, value_map, preferred_element_type=jnp.float32
    )
    slot_acc = jnp.einsum("gskjt,gstkd->gskjd", weights, values, precision=highest)
    hot_bool = seq_hot > 0
    hot_float = seq_hot.astype(jnp.float32)
    spread = jnp.where(hot_bool[None, :, None, None, :], slot_max[..., None], -1e30)
    seq_max = jnp.max(spread, axis=1)
    slot_seq_max = jnp.sum(
        jnp.where(hot_bool[None, :, None, None, :], seq_max[:, None], 0.0), axis=-1
    )
    factor = jnp.exp(slot_max - slot_seq_max)
    totals = jnp.einsum("gskj,sb->gkjb", slot_tot * factor, hot_float, precision=highest)
    accum = jnp.einsum(
        "gskjd,sb->gkjbd", slot_acc * factor[..., None], hot_float, precision=highest
    )
    return (seq_max, totals, accum)


def body(latent, up_key, up_value, queries, lengths, block_dest):
    groups = up_key.shape[0]
    dests = latent.shape[1]
    block_len = latent.shape[2]
    rank = latent.shape[3] // 2
    shards = block_dest.shape[0] // dests
    batch = queries.shape[0]
    q_heads = queries.shape[1]
    head_dim = queries.shape[2]
    per_group = up_key.shape[2] // head_dim
    per_kv = q_heads // (groups * per_group)
    blk_seq = block_dest.shape[0] // batch
    own_shard = lax.axis_index(SEQ)
    own_dests = lax.dynamic_slice_in_dim(block_dest, own_shard * dests, dests)
    source_order = (
        jnp.zeros((dests,), jnp.int32).at[own_dests].set(jnp.arange(dests, dtype=jnp.int32))
    )
    outgoing = latent[0][source_order]
    received = lax.all_to_all(outgoing, GRP_SEQ, split_axis=0, concat_axis=0, tiled=True)
    received = received.reshape(groups, shards, block_len, 2 * rank)
    decode_latent = received[None]
    key_map = up_key.reshape(groups, rank, per_group, head_dim)
    value_map = up_value.reshape(groups, rank, per_group, head_dim)
    query_rows = queries.reshape(batch, q_heads * head_dim)
    own_group = lax.axis_index("grp")
    slots = latent.shape[1]
    global_ids = own_shard * slots + jnp.arange(slots, dtype=jnp.int32)
    seq_hot, live = slot_info(global_ids, lengths, block_len, blk_seq, batch)
    picked = jnp.dot(seq_hot.astype(jnp.bfloat16), query_rows, preferred_element_type=jnp.float32)
    slot_query = picked.astype(jnp.bfloat16).reshape(slots, groups, per_group, per_kv, head_dim)
    group_query = lax.dynamic_slice_in_dim(slot_query, own_group, 1, 1)
    group_key = lax.dynamic_slice_in_dim(key_map, own_group, 1, 0)
    group_value = lax.dynamic_slice_in_dim(value_map, own_group, 1, 0)
    local = partials(latent, group_key, group_value, group_query, live, seq_hot)
    merged = joined_all(local, SEQ, combine)
    part_result = merged[2] / merged[1][..., None]
    result = lax.all_gather(part_result, "grp", axis=0, tiled=True)
    attended = jnp.transpose(result, (3, 0, 1, 2, 4)).reshape(batch, q_heads * head_dim)
    return (decode_latent, attended)


def solution(mesh):
    finer = Mesh(
        mesh.devices.reshape(mesh.shape["grp"], 4, 4, 2), ("grp", "seq_0", "seq_1", "seq_2")
    )
    in_specs = (P("grp", SEQ, None, None), P(), P(), P(), P(), P())
    out_specs = (P(GRP_SEQ, None, None, None, None), P())
    return jax.shard_map(body, mesh=finer, in_specs=in_specs, out_specs=out_specs, check_vma=False)
```

profile of v0, /device:TPU:0, one launch (start us, length us, event | category | flops | bytes accessed | tf_op | source)
XLA Modules:
  0.0 82.2 jit_solution(2277621008148799493)
XLA Ops:
  0.6 0.8 compare_select_fusion.1
  1.4 1.0 %scatter_custom_fusion = s32[128]{0:T(128)S(1)} fusion(s32[128]{0:T(128)S(1)} %compare_select_fusion.1, s32[128]{0:T(128)S(1)} %iota.27, s32[]{:T(128)} %constant.26.clone.1), kind=kCustom, calls=%fused_computation.172 | custom fusion | bytes 516 | tf_op jit(solution)/shard_map/scatter | solution.py:107
  2.4 3.6 %gather_fusion = bf16[128,32,256]{2,1,0:T(8,128)(2,1)} fusion(bf16[128,32,256]{2,1,0:T(8,128)(2,1)} %bitcast.358, s32[1024]{0:T(1024)S(1)} %pad_clamp_fusion), kind=kCustom, calls=%fused_computation | custom fusion | bytes 4194816 | tf_op jit(solution)/shard_map/gather | solution.py:109
  6.0 0.0 copy-start.4
  6.0 0.0 copy-start.1
  6.0 0.0 copy-start.2
  6.0 0.0 copy-start
  6.0 11.7 %all-to-all-start = ((bf16[128,32,256]{2,1,0:T(8,128)(2,1)}), bf16[128,32,256]{2,1,0:T(8,128)(2,1)}, u32[]{:S(2)}, u32[]{:S(2)}) async-start(bf16[128,32,256]{2,1,0:T(8,128)(2,1)} %gather_fusion), calls=%async_computation | async-start | bytes 4194304 | tf_op jit(solution)/shard_map/all_to_all | solution.py:110
  17.8 0.0 copy-done.4
  17.8 0.1 select_reduce_fusion.2
  17.9 0.0 copy-done.1
  17.9 0.1 reshape.1159
  17.9 0.0 copy-done.2
  17.9 0.1 reshape.1162
  18.0 0.1 constant_dynamic-slice_fusion
  18.1 0.0 copy-done
  18.1 0.0 copy-start.3
  18.1 0.7 fusion.14
  18.8 0.2 copy-done.3
  19.0 0.7 fusion.4
  19.8 0.6 copy.35
  20.4 0.1 add_compare_fusion
  20.5 3.6 %fusion.102 = (f32[128,2,8]{2,1,0:T(2,128)S(1)}, f32[128,2,8,32]{3,2,1,0:T(8,128)S(1)}) fusion(f32[2,128,128,32]{1,3,0,2:T(8,128)S(1)} %fusion.14, bf16[128,4,2,8,128]{4,3,2,1,0:T(8,128)(2,1)S(1)} %bitcast.359, s32[]{:T(128)S(6)} %select_n.72, pred[128,32]{1,0:T(8,128)(4,1)S(1)} %add_compare_fusion), kind=kOutput, calls=%fused_computation.176 | convolution fusion | flops 100857856 | bytes 5005316 | tf_op jit(solution)/shard_map/gstkd,sgkjd->gskjt/dot_general | solution.py:65
  24.2 0.1 copy.25
  24.2 0.1 select_reduce_fusion.1
  24.3 0.1 select_reduce_fusion
  24.4 0.1 reshape.1166
  24.5 0.1 copy.26
  24.7 0.7 convolution_bitcast_fusion
  25.4 0.8 fusion.21
  26.2 3.7 %fusion.5 = f32[128,2,8,128]{3,2,1,0:T(8,128)S(1)} fusion(f32[128,32,2,128]{3,1,0,2:T(8,128)S(1)} %convolution_bitcast_fusion, f32[128,2,8,32]{3,2,1,0:T(8,128)S(1)} %get-tuple-element.30, f32[128,2,8]{2,1,0:T(2,128)S(1)} %copy.26, f32[128,2,8]{2,1,0:T(2,128)S(1)} %get-tuple-element.29, pred[128,32]{1,0:T(8,128)(4,1)S(1)} %add_compare_fusion), kind=kOutput, calls=%fused_computation.9 | convolution fusion | flops 101056512 | bytes 5525504 | tf_op jit(solution)/shard_map/gskjt,gstkd->gskjd/dot_general | solution.py:76
  29.9 0.9 %fusion.17 = f32[8,2,8,128]{3,0,2,1:T(8,128)S(1)} fusion(f32[128,2,8,128]{3,2,1,0:T(8,128)S(1)} %fusion.5, s32[128]{0:T(128)S(1)} %get-tuple-element.31), kind=kOutput, calls=%fused_computation.15 | convolution fusion | flops 25168896 | bytes 1114624 | tf_op jit(solution)/shard_map/gskjd,sb->gkjbd/dot_general | solution.py:86
  30.7 0.1 copy.28
  30.8 0.1 fusion.49
  30.9 0.1 reshape.1167
  31.1 18.3 %all-gather.3 = f32[4,130,128]{2,1,0:T(8,128)S(1)} all-gather(f32[1,130,128]{2,1,0:T(8,128)S(1)} %maximum_bitcast_fusion), channel_id=2, replica_groups=mesh['grp'=4,'seq_0'=4,'seq_1'=4,'seq_2'=2] {'seq_0'}, dimensions={0}, use_global_device_ids=true | all-gather | bytes 332800 | tf_op jit(solution)/shard_map/all_gather | solution.py:19
  49.4 0.2 fusion.39
  49.6 12.7 %all-gather.4 = f32[4,130,128]{2,1,0:T(8,128)S(1)} all-gather(f32[1,130,128]{2,1,0:T(8,128)S(1)} %maximum_bitcast_fusion.1), channel_id=3, replica_groups=mesh['grp'=4,'seq_0'=4,'seq_1'=4,'seq_2'=2] {'seq_1'}, dimensions={0}, use_global_device_ids=true | all-gather | bytes 332800 | tf_op jit(solution)/shard_map/all_gather | solution.py:19
  62.4 0.2 fusion.30
  62.6 1.9 %all-gather.5 = f32[2,130,128]{2,1,0:T(8,128)S(1)} all-gather(f32[1,130,128]{2,1,0:T(8,128)S(1)} %maximum_bitcast_fusion.2), channel_id=4, replica_groups=mesh['grp'=4,'seq_0'=4,'seq_1'=4,'seq_2'=2] {'seq_2'}, dimensions={0}, use_global_device_ids=true | all-gather | bytes 199680 | tf_op jit(solution)/shard_map/all_gather | solution.py:19
  64.5 0.1 squeeze.143
  64.6 0.1 squeeze.144
  64.7 0.1 squeeze.146
  64.8 0.1 squeeze.147
  64.9 0.1 add_divide_fusion
  65.0 13.4 %all_gather.27 = f32[4,2,8,8,128]{4,3,2,1,0:T(8,128)S(1)} all-gather(f32[1,2,8,8,128]{4,3,2,1,0:T(8,128)S(1)} %add_divide_fusion), channel_id=1, replica_groups=mesh['grp'=4,'seq_0'=4,'seq_1'=4,'seq_2'=2] {'grp'}, dimensions={0}, use_global_device_ids=true | all-gather | bytes 327680 | tf_op jit(solution)/shard_map/all_gather | solution.py:128
  78.4 0.0 all-to-all-done
  78.4 3.1 %copy.52 = bf16[1,4,32,32,256]{4,3,2,1,0:T(8,128)(2,1)} copy(bf16[1,4,32,32,256]{4,3,2,1,0:T(8,128)(2,1)} %bitcast.1) | data formatting | bytes 4194304
  81.5 0.7 copy.53
  (18 shorter events, 0.2 us)
Async XLA Ops:
  6.0 11.8 %copy-start.4 = (s32[8]{0:T(128)S(1)}, s32[8]{0:T(128)}, u32[]{:S(2)}) copy-start(s32[8]{0:T(128)} %param.10) | copy-start | bytes 100
  6.0 11.9 %copy-start.1 = (bf16[4,128,256]{2,1,0:T(8,128)(2,1)S(1)}, bf16[4,128,256]{2,1,0:T(8,128)(2,1)}, u32[]{:S(2)}) copy-start(bf16[4,128,256]{2,1,0:T(8,128)(2,1)} %param.7) | copy-start | bytes 786436
  6.0 11.9 %copy-start.2 = (bf16[4,128,256]{2,1,0:T(8,128)(2,1)S(1)}, bf16[4,128,256]{2,1,0:T(8,128)(2,1)}, u32[]{:S(2)}) copy-start(bf16[4,128,256]{2,1,0:T(8,128)(2,1)} %param.8) | copy-start | bytes 786436
  6.0 12.1 %copy-start = (bf16[1,128,32,256]{3,2,1,0:T(8,128)(2,1)S(1)}, bf16[1,128,32,256]{3,2,1,0:T(8,128)(2,1)}, u32[]{:S(2)}) copy-start(bf16[1,128,32,256]{3,2,1,0:T(8,128)(2,1)} %param.6) | copy-start | bytes 6291460
  6.0 72.4 %all-to-all-start = ((bf16[128,32,256]{2,1,0:T(8,128)(2,1)}), bf16[128,32,256]{2,1,0:T(8,128)(2,1)}, u32[]{:S(2)}, u32[]{:S(2)}) async-start(bf16[128,32,256]{2,1,0:T(8,128)(2,1)} %gather_fusion), calls=%async_computation | async-start | bytes 4194304 | tf_op jit(solution)/shard_map/all_to_all | solution.py:110
  18.1 0.9 %copy-start.3 = (bf16[8,64,128]{2,1,0:T(8,128)(2,1)S(1)}, bf16[8,64,128]{2,1,0:T(8,128)(2,1)}, u32[]{:S(2)}) copy-start(bf16[8,64,128]{2,1,0:T(8,128)(2,1)} %param.9) | copy-start | bytes 393220
where the time goes:
time: 82.5 us; the launch traced here: 82.2 us
  blocking collectives  46.3 us (56%)
  starting transfers between devices  11.7 us (14%)
  matrix products  10.4 us (13%)
  local copies, waits for them, and re-layouts  10.2 us (12%)
  other arithmetic  2.58 us (3%)
  between operations  0.89 us (1%)
    all_gather x3, blocking collectives, all_in_one(): both, at, found = (lax.all_gather(jnp.concatenate(lines), axis), 0, {})  32.9 us
    all_gather x1, blocking collectives, body(): result = lax.all_gather(part_result, 'grp', axis=0, tiled=True)  13.4 us
    all_to_all x1, starting transfers between devices, body(): lax.all_to_all(outgoing, GRP_SEQ, split_axis=0, concat_axis=0, tiled=True)  11.7 us
    unnamed x13, local copies, waits for them, and re-layouts  4.61 us
    dot_general x1, matrix products, partials(): jnp.einsum('gskjt,gstkd->gskjd', weights, values, precision=highest)  3.68 us
    dot_general x1, matrix products, partials(): jnp.einsum('gstkd,sgkjd->gskjt', keys, slot_query.astype(jnp.float32), pr...  3.63 us
    gather x1, local copies, waits for them, and re-layouts, body(): outgoing = latent[0][source_order]  3.59 us
  transfers between devices with their start and end apart: 1, of which 0 were waited for; matrix products, arithmetic and copies ran while one was open for 17% of the time, Pallas kernels for 0%

commit v1 on v0

--- a/solution.py
+++ b/solution.py
@@ -6,6 +6,12 @@
 
 SEQ = ("seq_0", "seq_1", "seq_2")
 GRP_SEQ = ("grp", "seq_0", "seq_1", "seq_2")
+
+
+def in_order(tiles, dim):
+    shape = list(tiles.shape[1:])
+    shape[dim] *= tiles.shape[0]
+    return jnp.moveaxis(tiles, 0, dim).reshape(shape)
 
 
 def all_in_one(x, axis):
@@ -125,7 +131,19 @@
     local = partials(latent, group_key, group_value, group_query, live, seq_hot)
     merged = joined_all(local, SEQ, combine)
     part_result = merged[2] / merged[1][..., None]
-    result = lax.all_gather(part_result, "grp", axis=0, tiled=True)
+    size = lax.axis_size("grp")
+    pairs = [(i, (i + 1) % size) for i in range(size)]
+    back = [(b, a) for a, b in pairs]
+    lower, upper = ([], [])
+    for step in range(size - 1):
+        if step % 2 == 0:
+            lower.append(lax.ppermute(lower[-1] if lower else part_result, "grp", pairs))
+        else:
+            upper.append(lax.ppermute(upper[-1] if upper else part_result, "grp", back))
+    blocks = jnp.stack([*lower[::-1], part_result, *upper])
+    shift = lax.axis_index("grp") - len(lower)
+    blocks = blocks[(jnp.arange(size) - shift) % size]
+    result = in_order(blocks, 0)
     attended = jnp.transpose(result, (3, 0, 1, 2, 4)).reshape(batch, q_heads * head_dim)
     return (decode_latent, attended)
 

time: 82.5 us -> 81.4 us (0.987)
  blocking collectives: 46.3 us -> 32.9 us
  waiting for transfers between devices: 0.01 us -> 7.65 us
  starting transfers between devices: 11.7 us -> 15.6 us
    all_gather x1 -> x0, blocking collectives: 13.4 us -> none  [body(): result = lax.all_gather(part_result, 'grp', axis=0, tiled=True)]
    ppermute x0 -> x3, waiting for transfers between devices: none -> 7.65 us  [the longest x2 7.65 us: body(): lax.ppermute(lower[-1] if lower else part_result, 'grp', pairs)]
    ppermute x0 -> x3, starting transfers between devices: none -> 3.92 us  [the longest x1 2.01 us: body(): upper.append(lax.ppermute(upper[-1] if upper else part_result, 'grp', back))]
    gather x0 -> x1, local copies, waits for them, and re-layouts: none -> 1.27 us  [body(): blocks = blocks[(jnp.arange(size) - shift) % size]]
    unnamed x13 -> x12, local copies, waits for them, and re-layouts: 4.61 us -> 3.91 us
  transfers between devices with their start and end apart: 1 -> 4, of which waited for: 0 -> 2; matrix products, arithmetic and copies ran while one was open for 17% -> 19% of each run, Pallas kernels for 0% -> 0%
where the time goes in v1:
time: 81.4 us; the launch traced here: 81.1 us
  blocking collectives  32.9 us (40%)
  starting transfers between devices  15.6 us (19%)
  local copies, waits for them, and re-layouts  10.8 us (13%)
  matrix products  10.4 us (13%)
  waiting for transfers between devices  7.65 us (9%)
  other arithmetic  2.75 us (3%)
  between operations  0.92 us (1%)
    all_gather x3, blocking collectives, all_in_one(): both, at, found = (lax.all_gather(jnp.concatenate(lines), axis), 0, {})  32.9 us
    all_to_all x1, starting transfers between devices, body(): lax.all_to_all(outgoing, GRP_SEQ, split_axis=0, concat_axis=0, tiled=True)  11.7 us
    ppermute x2, waiting for transfers between devices, body(): lax.ppermute(lower[-1] if lower else part_result, 'grp', pairs)  7.65 us
    unnamed x12, local copies, waits for them, and re-layouts  3.91 us
    dot_general x1, matrix products, partials(): jnp.einsum('gskjt,gstkd->gskjd', weights, values, precision=highest)  3.68 us
    dot_general x1, matrix products, partials(): jnp.einsum('gstkd,sgkjd->gskjt', keys, slot_query.astype(jnp.float32), pr...  3.63 us
    gather x1, local copies, waits for them, and re-layouts, body(): outgoing = latent[0][source_order]  3.59 us
    ppermute x1, starting transfers between devices, body(): upper.append(lax.ppermute(upper[-1] if upper else part_result, 'grp', back))  2.01 us
  transfers between devices with their start and end apart: 4, of which 2 were waited for; matrix products, arithmetic and copies ran while one was open for 19% of the time, Pallas kernels for 0%

profile of v1, /device:TPU:0, one launch (start us, length us, event | category | flops | bytes accessed | tf_op | source)
XLA Modules:
  0.0 81.1 jit_solution(7289924709529206571)
XLA Ops:
  0.6 0.8 compare_select_fusion.2
  1.4 1.0 %scatter_custom_fusion = s32[128]{0:T(128)S(1)} fusion(s32[128]{0:T(128)S(1)} %compare_select_fusion.2, s32[128]{0:T(128)S(1)} %iota.31, s32[]{:T(128)} %constant.63.clone.1), kind=kCustom, calls=%fused_computation.182 | custom fusion | bytes 516 | tf_op jit(solution)/shard_map/scatter | solution.py:113
  2.4 3.6 %gather_fusion = bf16[128,32,256]{2,1,0:T(8,128)(2,1)} fusion(bf16[128,32,256]{2,1,0:T(8,128)(2,1)} %bitcast.367, s32[1024]{0:T(1024)S(1)} %pad_clamp_fusion.1), kind=kCustom, calls=%fused_computation | custom fusion | bytes 4194816 | tf_op jit(solution)/shard_map/gather | solution.py:115
  6.0 0.0 copy-start.4
  6.0 0.0 copy-start.1
  6.0 0.0 copy-start.2
  6.0 0.0 copy-start
  6.0 11.7 %all-to-all-start = ((bf16[128,32,256]{2,1,0:T(8,128)(2,1)}), bf16[128,32,256]{2,1,0:T(8,128)(2,1)}, u32[]{:S(2)}, u32[]{:S(2)}) async-start(bf16[128,32,256]{2,1,0:T(8,128)(2,1)} %gather_fusion), calls=%async_computation | async-start | bytes 4194304 | tf_op jit(solution)/shard_map/all_to_all | solution.py:116
  17.8 0.0 copy-done.4
  17.8 0.1 select_reduce_fusion.2
  17.9 0.0 copy-done.1
  17.9 0.1 reshape.1237
  17.9 0.0 copy-done.2
  17.9 0.1 reshape.1240
  18.0 0.1 constant_dynamic-slice_fusion
  18.1 0.0 copy-done
  18.1 0.0 copy-start.3
  18.1 0.7 fusion.14
  18.8 0.2 copy-done.3
  19.0 0.7 fusion.4
  19.8 0.6 copy.35
  20.4 0.1 add_compare_fusion
  20.5 3.6 %fusion.104 = (f32[128,2,8]{2,1,0:T(2,128)S(1)}, f32[128,2,8,32]{3,2,1,0:T(8,128)S(1)}) fusion(f32[2,128,128,32]{1,3,0,2:T(8,128)S(1)} %fusion.14, bf16[128,4,2,8,128]{4,3,2,1,0:T(8,128)(2,1)S(1)} %bitcast.368, s32[]{:T(128)S(6)} %select_n.95, pred[128,32]{1,0:T(8,128)(4,1)S(1)} %add_compare_fusion), kind=kOutput, calls=%fused_computation.186 | convolution fusion | flops 100857856 | bytes 5005316 | tf_op jit(solution)/shard_map/gstkd,sgkjd->gskjt/dot_general | solution.py:71
  24.2 0.1 copy.25
  24.2 0.1 select_reduce_fusion.1
  24.3 0.1 select_reduce_fusion
  24.4 0.1 reshape.1244
  24.5 0.1 copy.26
  24.7 0.7 convolution_bitcast_fusion
  25.4 0.8 fusion.21
  26.2 3.7 %fusion.5 = f32[128,2,8,128]{3,2,1,0:T(8,128)S(1)} fusion(f32[128,32,2,128]{3,1,0,2:T(8,128)S(1)} %convolution_bitcast_fusion, f32[128,2,8,32]{3,2,1,0:T(8,128)S(1)} %get-tuple-element.30, f32[128,2,8]{2,1,0:T(2,128)S(1)} %copy.26, f32[128,2,8]{2,1,0:T(2,128)S(1)} %get-tuple-element.29, pred[128,32]{1,0:T(8,128)(4,1)S(1)} %add_compare_fusion), kind=kOutput, calls=%fused_computation.10 | convolution fusion | flops 101056512 | bytes 5525504 | tf_op jit(solution)/shard_map/gskjt,gstkd->gskjd/dot_general | solution.py:82
  29.9 0.9 %fusion.17 = f32[8,2,8,128]{3,0,2,1:T(8,128)S(1)} fusion(f32[128,2,8,128]{3,2,1,0:T(8,128)S(1)} %fusion.5, s32[128]{0:T(128)S(1)} %get-tuple-element.31), kind=kOutput, calls=%fused_computation.16 | convolution fusion | flops 25168896 | bytes 1114624 | tf_op jit(solution)/shard_map/gskjd,sb->gkjbd/dot_general | solution.py:92
  30.7 0.1 copy.28
  30.8 0.1 fusion.49
  30.9 0.1 reshape.1245
  31.1 18.3 %all-gather.3 = f32[4,130,128]{2,1,0:T(8,128)S(1)} all-gather(f32[1,130,128]{2,1,0:T(8,128)S(1)} %maximum_bitcast_fusion.1), channel_id=2, replica_groups=mesh['grp'=4,'seq_0'=4,'seq_1'=4,'seq_2'=2] {'seq_0'}, dimensions={0}, use_global_device_ids=true | all-gather | bytes 332800 | tf_op jit(solution)/shard_map/all_gather | solution.py:25
  49.4 0.2 fusion.39
  49.6 12.7 %all-gather.4 = f32[4,130,128]{2,1,0:T(8,128)S(1)} all-gather(f32[1,130,128]{2,1,0:T(8,128)S(1)} %maximum_bitcast_fusion.2), channel_id=3, replica_groups=mesh['grp'=4,'seq_0'=4,'seq_1'=4,'seq_2'=2] {'seq_1'}, dimensions={0}, use_global_device_ids=true | all-gather | bytes 332800 | tf_op jit(solution)/shard_map/all_gather | solution.py:25
  62.4 0.2 fusion.30
  62.6 1.9 %all-gather.5 = f32[2,130,128]{2,1,0:T(8,128)S(1)} all-gather(f32[1,130,128]{2,1,0:T(8,128)S(1)} %maximum_bitcast_fusion.3), channel_id=4, replica_groups=mesh['grp'=4,'seq_0'=4,'seq_1'=4,'seq_2'=2] {'seq_2'}, dimensions={0}, use_global_device_ids=true | all-gather | bytes 199680 | tf_op jit(solution)/shard_map/all_gather | solution.py:25
  64.5 0.1 squeeze.147
  64.6 0.1 squeeze.148
  64.7 0.1 squeeze.150
  64.8 0.1 squeeze.151
  64.9 0.1 add_divide_fusion.1
  65.0 1.9 %collective-permute-start = (f32[1,2,8,8,128]{4,3,2,1,0:T(8,128)S(1)}, f32[1,2,8,8,128]{4,3,2,1,0:T(8,128)S(1)}, u32[]{:S(2)}, u32[]{:S(2)}) collective-permute-start(f32[1,2,8,8,128]{4,3,2,1,0:T(8,128)S(1)} %add_divide_fusion.1), channel_id=1, source_target_pairs={{0,32},{32,64},{64,96},{96,0},{1,33},{33,65},{65,97},{97,1},{2,34}... | collective-permute-start | bytes 196616 | tf_op jit(solution)/shard_map/ppermute | solution.py:140
  66.9 2.0 %collective-permute-start.2 = (f32[1,2,8,8,128]{4,3,2,1,0:T(8,128)S(1)}, f32[1,2,8,8,128]{4,3,2,1,0:T(8,128)S(1)}, u32[]{:S(2)}, u32[]{:S(2)}) collective-permute-start(f32[1,2,8,8,128]{4,3,2,1,0:T(8,128)S(1)} %add_divide_fusion.1), channel_id=1, source_target_pairs={{32,0},{64,32},{96,64},{0,96},{33,1},{65,33},{97,65},{1,97},{34,2}... | collective-permute-start | bytes 196616 | tf_op jit(solution)/shard_map/ppermute | solution.py:142
  68.9 0.1 add_divide_fusion
  69.1 2.2 %collective-permute-done = f32[1,2,8,8,128]{4,3,2,1,0:T(8,128)S(1)} collective-permute-done((f32[1,2,8,8,128]{4,3,2,1,0:T(8,128)S(1)}, f32[1,2,8,8,128]{4,3,2,1,0:T(8,128)S(1)}, u32[]{:S(2)}, u32[]{:S(2)}) %collective-permute-start) | collective-permute-done | bytes 65568 | tf_op jit(solution)/shard_map/ppermute | solution.py:140
  71.3 0.0 collective-permute-start.1
  71.3 0.0 collective-permute-done.2
  71.3 5.5 %collective-permute-done.1 = f32[1,2,8,8,128]{4,3,2,1,0:T(8,128)S(1)} collective-permute-done((f32[1,2,8,8,128]{4,3,2,1,0:T(8,128)S(1)}, f32[1,2,8,8,128]{4,3,2,1,0:T(8,128)S(1)}, u32[]{:S(2)}, u32[]{:S(2)}) %collective-permute-start.1) | collective-permute-done | bytes 65568 | tf_op jit(solution)/shard_map/ppermute | solution.py:140
  76.8 1.3 %gather_fusion.1 = f32[4,2,8,8,128]{4,3,2,1,0:T(8,128)} fusion(f32[4,2,8,8,128]{4,3,2,1,0:T(8,128)S(1)} %maximum_bitcast_fusion, s32[1024]{0:T(1024)S(1)} %pad_clamp_fusion), kind=kCustom, calls=%fused_computation.1 | custom fusion | bytes 524304 | tf_op jit(solution)/shard_map/gather | solution.py:145
  78.0 0.0 all-to-all-done
  78.0 3.1 %copy.51 = bf16[1,4,32,32,256]{4,3,2,1,0:T(8,128)(2,1)} copy(bf16[1,4,32,32,256]{4,3,2,1,0:T(8,128)(2,1)} %bitcast.1) | data formatting | bytes 4194304
  (21 shorter events, 0.2 us)
Async XLA Ops:
  6.0 11.8 %copy-start.4 = (s32[8]{0:T(128)S(1)}, s32[8]{0:T(128)}, u32[]{:S(2)}) copy-start(s32[8]{0:T(128)} %param.10) | copy-start | bytes 100
  6.0 11.9 %copy-start.1 = (bf16[4,128,256]{2,1,0:T(8,128)(2,1)S(1)}, bf16[4,128,256]{2,1,0:T(8,128)(2,1)}, u32[]{:S(2)}) copy-start(bf16[4,128,256]{2,1,0:T(8,128)(2,1)} %param.7) | copy-start | bytes 786436
  6.0 11.9 %copy-start.2 = (bf16[4,128,256]{2,1,0:T(8,128)(2,1)S(1)}, bf16[4,128,256]{2,1,0:T(8,128)(2,1)}, u32[]{:S(2)}) copy-start(bf16[4,128,256]{2,1,0:T(8,128)(2,1)} %param.8) | copy-start | bytes 786436
  6.0 12.1 %copy-start = (bf16[1,128,32,256]{3,2,1,0:T(8,128)(2,1)S(1)}, bf16[1,128,32,256]{3,2,1,0:T(8,128)(2,1)}, u32[]{:S(2)}) copy-start(bf16[1,128,32,256]{3,2,1,0:T(8,128)(2,1)} %param.6) | copy-start | bytes 6291460
  6.0 72.0 %all-to-all-start = ((bf16[128,32,256]{2,1,0:T(8,128)(2,1)}), bf16[128,32,256]{2,1,0:T(8,128)(2,1)}, u32[]{:S(2)}, u32[]{:S(2)}) async-start(bf16[128,32,256]{2,1,0:T(8,128)(2,1)} %gather_fusion), calls=%async_computation | async-start | bytes 4194304 | tf_op jit(solution)/shard_map/all_to_all | solution.py:116
  18.1 0.9 %copy-start.3 = (bf16[8,64,128]{2,1,0:T(8,128)(2,1)S(1)}, bf16[8,64,128]{2,1,0:T(8,128)(2,1)}, u32[]{:S(2)}) copy-start(bf16[8,64,128]{2,1,0:T(8,128)(2,1)} %param.9) | copy-start | bytes 393220
  65.0 6.3 %collective-permute-start = (f32[1,2,8,8,128]{4,3,2,1,0:T(8,128)S(1)}, f32[1,2,8,8,128]{4,3,2,1,0:T(8,128)S(1)}, u32[]{:S(2)}, u32[]{:S(2)}) collective-permute-start(f32[1,2,8,8,128]{4,3,2,1,0:T(8,128)S(1)} %add_divide_fusion.1), channel_id=1, source_target_pairs={{0,32},{32,64},{64,96},{96,0},{1,33},{33,65},{65,97},{97,1},{2,34}... | collective-permute-start | bytes 196616 | tf_op jit(solution)/shard_map/ppermute | solution.py:140
  66.9 4.4 %collective-permute-start.2 = (f32[1,2,8,8,128]{4,3,2,1,0:T(8,128)S(1)}, f32[1,2,8,8,128]{4,3,2,1,0:T(8,128)S(1)}, u32[]{:S(2)}, u32[]{:S(2)}) collective-permute-start(f32[1,2,8,8,128]{4,3,2,1,0:T(8,128)S(1)} %add_divide_fusion.1), channel_id=1, source_target_pairs={{32,0},{64,32},{96,64},{0,96},{33,1},{65,33},{97,65},{1,97},{34,2}... | collective-permute-start | bytes 196616 | tf_op jit(solution)/shard_map/ppermute | solution.py:142
  71.3 5.5 %collective-permute-start.1 = (f32[1,2,8,8,128]{4,3,2,1,0:T(8,128)S(1)}, f32[1,2,8,8,128]{4,3,2,1,0:T(8,128)S(1)}, u32[]{:S(2)}, u32[]{:S(2)}) collective-permute-start(f32[1,2,8,8,128]{4,3,2,1,0:T(8,128)S(1)} %collective-permute-done), channel_id=1, source_target_pairs={{0,32},{32,64},{64,96},{96,0},{1,33},{33,65},{65,97},{97,1},{2,34}... | collective-permute-start | bytes 196616 | tf_op jit(solution)/shard_map/ppermute | solution.py:140
